TPU v7x, 32 devices: a whole 2x2x4 slice. The times are simulated.
32 devices in a mesh: hist: 4 (over z), rows: 2 (over y), dom: 4 (over x, core).
Axes of the slice: x: 2, y: 2, z: 4, core: 2. Of those that a mesh axis runs over, the one named last changes fastest.
Arguments:
- row_index: int32 [4, 32768], P(None, ('hist', 'rows', 'dom')), may hold values from 0 to 510
- col_index: int32 [4, 32768], P(None, ('hist', 'rows', 'dom')), may hold values from 0 to 510
- bin_index: int32 [4, 32768], P(None, ('hist', 'rows', 'dom')), may hold values from 0 to 255
- charge: bfloat16 [32768], P(('hist', 'rows', 'dom')), may hold values from 0.5 to 2
- momentum: float32 [2, 32768], P(None, ('hist', 'rows', 'dom')), may hold values from -6 to 6
- history: bfloat16 [32, 512, 512], P('hist', 'rows'), may hold values from 0 to 2
- kernel_cols: bfloat16 [32, 512, 512], P('hist', 'dom'), may hold values from -0.25 to 0.25
- kernel_rows: bfloat16 [32, 512, 2, 512], P('hist', 'rows'), may hold values from -0.046875 to 0.046875
Outputs:
- momentum_out: float32 [2, 32768], P(None, ('hist', 'rows', 'dom'))
- history_out: bfloat16 [32, 512, 512], P('hist', 'rows')
All inputs are finite; a program needn't handle non-finite values.
Results may differ from a plain program's by a relative error of at most 0.0024.
Values may be sent and summed in bfloat16 or wider, within the bound.
A program may use at most 64 MiB of HBM per device.

v0:
```python
import jax
import jax.numpy as jnp
from jax import lax
from jax.sharding import PartitionSpec as P

NG = 512
BINS = 16
STEPS = 4


kick_scale = 0.5


def from_behind(array, axis, by):
    size = lax.axis_size(axis)
    pairs = [(i, i + by) for i in range(size) if 0 <= i + by < size]
    return lax.ppermute(array, axis, pairs)


def tables(cell_index, fraction, extent):
    places = lax.broadcasted_iota(jnp.int32, (cell_index.shape[0], extent), 1)
    lower = jnp.where(places == cell_index[:, None], (1.0 - fraction)[:, None], 0.0)
    return lower + jnp.where(places == cell_index[:, None] + 1, fraction[:, None], 0.0)


def local(row_index, col_index, bin_index, charge, momentum, history, kernel_cols, kernel_rows):
    band_rows = history.shape[1]
    charge_f = charge.astype(jnp.float32)
    cycle_now = history
    kick_sum = jnp.zeros((charge.shape[0], 2), jnp.float32)
    contract_first = (((0,), (0,)), ((), ()))
    for turn_index in range(STEPS):
        bin_now = bin_index[turn_index]
        frac_row = ((bin_now // BINS).astype(jnp.float32) + 0.5) / BINS
        frac_col = ((bin_now % BINS).astype(jnp.float32) + 0.5) / BINS
        row_plain = tables(row_index[turn_index], frac_row, NG)
        row_charged = (row_plain * charge_f[:, None]).astype(jnp.bfloat16)
        row_table = row_plain.astype(jnp.bfloat16)
        col_plain = tables(col_index[turn_index], frac_col, NG)
        col_table = col_plain.astype(jnp.bfloat16)
        partial_grid = lax.dot_general(
            row_charged, col_table, contract_first, preferred_element_type=jnp.float32
        )
        whole_grid = lax.psum(partial_grid, ("hist", "rows", "dom"))
        grid_rows = lax.dynamic_slice_in_dim(
            whole_grid, lax.axis_index("rows") * band_rows, band_rows, 0
        )
        newest = grid_rows.astype(jnp.bfloat16)
        incoming = from_behind(cycle_now[-1], "hist", 1)
        leading = jnp.where(lax.axis_index("hist") == 0, newest, incoming)
        cycle_now = jnp.concatenate([leading[None], cycle_now[:-1]], axis=0)
        mixed_rows = jnp.einsum(
            "kab,kjb->kaj", cycle_now, kernel_cols, preferred_element_type=jnp.float32
        ).astype(jnp.bfloat16)
        partial_field = jnp.einsum(
            "kaci,kaj->icj", kernel_rows, mixed_rows, preferred_element_type=jnp.float32
        )
        summed = lax.psum(partial_field, ("hist", "rows")).astype(jnp.bfloat16)
        field_full = lax.all_gather(summed, "dom", axis=2, tiled=True)
        along_rows = jnp.dot(
            row_table, field_full.reshape(NG, 2 * NG), preferred_element_type=jnp.float32
        )
        kick_now = jnp.sum(along_rows.reshape(-1, 2, NG) * col_plain[:, None, :], axis=2)
        kick_sum = kick_sum + kick_now
    momentum_out = momentum + kick_scale * kick_sum.T
    return (momentum_out, cycle_now)


def solution(mesh):
    in_specs = (
        P(None, ("hist", "rows", "dom")),
        P(None, ("hist", "rows", "dom")),
        P(None, ("hist", "rows", "dom")),
        P(("hist", "rows", "dom")),
        P(None, ("hist", "rows", "dom")),
        P("hist", "rows", None),
        P("hist", "dom", None),
        P("hist", "rows", None, None),
    )
    out_specs = (P(None, ("hist", "rows", "dom")), P("hist", "rows", None))
    return jax.shard_map(local, mesh=mesh, in_specs=in_specs, out_specs=out_specs, check_vma=False)
```

profile of v0, /device:TPU:0, one launch (start us, length us, event | category | flops | bytes accessed | tf_op | source)
XLA Modules:
  0.0 326.2 jit_solution(7703502074887815081)
XLA Ops:
  7.2 0.0 copy-start
  7.2 0.0 copy-start.8
  7.2 0.0 copy-start.9
  7.2 0.0 copy-start.10
  7.2 0.0 copy-start.12
  7.2 0.0 all-gather.7.cloned.1.call-start
  7.3 2.3 slice_bitcast_fusion
  9.6 5.6 %collective-permute-start = (bf16[256,512]{1,0:T(8,128)(2,1)}, bf16[256,512]{1,0:T(8,128)(2,1)}, u32[]{:S(2)}, u32[]{:S(2)}) collective-permute-start(bf16[256,512]{1,0:T(8,128)(2,1)} %get-tuple-element.28), channel_id=1, source_target_pairs={{0,8},{8,16},{16,24},{1,9},{9,17},{17,25},{2,10},{10,18},{18,26},{... | collective-permute-start | bytes 786440 | tf_op jit(solution)/shard_map/ppermute | solution.py:17
  15.2 2.8 collective-permute-start.1
  18.0 4.2 %collective-permute-start.2 = (bf16[256,512]{1,0:T(8,128)(2,1)}, bf16[256,512]{1,0:T(8,128)(2,1)}, u32[]{:S(2)}, u32[]{:S(2)}) collective-permute-start(bf16[256,512]{1,0:T(8,128)(2,1)} %get-tuple-element.29), channel_id=1, source_target_pairs={{0,8},{8,16},{16,24},{1,9},{9,17},{17,25},{2,10},{10,18},{18,26},{... | collective-permute-start | bytes 786440 | tf_op jit(solution)/shard_map/ppermute | solution.py:17
  22.2 2.0 collective-permute-start.3
  24.2 0.0 copy-done.8
  24.2 0.0 copy-done.9
  24.2 0.0 copy-done.10
  24.3 0.0 copy-done.12
  24.3 2.0 fusion.58
  26.4 2.0 fusion.59
  28.4 3.0 fusion.60
  31.4 3.0 fusion.61
  34.5 91.2 %all-reduce.4 = (bf16[512,512]{1,0:T(8,128)(2,1)}, bf16[512,512]{1,0:T(8,128)(2,1)}, bf16[512,512]{1,0:T(8,128)(2,1)}, bf16[512,512]{1,0:T(8,128)(2,1)}) all-reduce(f32[512,512]{1,0:T(8,128)} %fusion.60, f32[512,512]{1,0:T(8,128)S(1)} %fusion.59, ...), channel_id=1, replica_groups=mesh['hist'=4,'rows'=2,'dom'=4] {'hist','rows','dom'}, use_global_device_ids=true, to_apply=%region_6.7 | all-reduce | flops 1048576 | bytes 6291456 | tf_op jit(solution)/shard_map/psum | solution.py:44
  125.7 1.6 slice.73
  127.3 0.0 collective-permute-done
  127.3 1.0 fusion.129
  128.4 0.0 collective-permute-done.1
  128.4 0.0 copy-start.7
  128.4 0.7 copy-done.7
  129.1 1.0 fusion.131
  130.1 0.0 copy-done
  130.1 4.4 %fusion.46 = f32[512,2,128]{0,2,1:T(8,128)} fusion(bf16[8,256,2,512]{3,2,1,0:T(2,128)(2,1)} %param.15, bf16[8,128,512]{2,1,0:T(8,128)(2,1)S(1)} %copy-done, bf16[7,256,512]{2,1,0:T(8,128)(2,1)S(1)} %slice.73, bf16[1,256,512]{2,1,0:T(8,128)(2,1)S(1)} %fusion.129, bf16[1,256,512]{2,1,0:T(8,128)(2,1)S(1)} %fusion.131), kind=kOutput, calls=%fused_computation.71 | convolution fusion | flops 807665664 | bytes 8126464 | tf_op jit(solution)/shard_map/kaci,kaj->icj/dot_general | solution.py:55
  134.5 0.0 collective-permute-done.2
  134.5 1.7 fusion.133
  136.2 4.4 %fusion.49 = f32[512,2,128]{0,2,1:T(8,128)} fusion(bf16[8,256,2,512]{3,2,1,0:T(2,128)(2,1)} %param.15, bf16[8,128,512]{2,1,0:T(8,128)(2,1)S(1)} %copy-done, bf16[1,256,512]{2,1,0:T(8,128)(2,1)S(1)} %fusion.131, bf16[7,256,512]{2,1,0:T(8,128)(2,1)S(1)} %slice.73, bf16[1,256,512]{2,1,0:T(8,128)(2,1)S(1)} %fusion.129, bf16[1,256,512]{2,1,0:T(8,128)(2,1)} %fusion.133), kind=kOutput, calls=%fused_computation.72 | convolution fusion | flops 808714240 | bytes 8388608 | tf_op jit(solution)/shard_map/kaci,kaj->icj/dot_general | solution.py:55
  140.7 4.4 %fusion.43 = f32[512,2,128]{0,2,1:T(8,128)} fusion(bf16[8,256,2,512]{3,2,1,0:T(2,128)(2,1)} %param.15, bf16[8,128,512]{2,1,0:T(8,128)(2,1)S(1)} %copy-done, bf16[7,256,512]{2,1,0:T(8,128)(2,1)S(1)} %slice.73, bf16[1,256,512]{2,1,0:T(8,128)(2,1)S(1)} %fusion.129), kind=kOutput, calls=%fused_computation.70 | convolution fusion | flops 806617088 | bytes 7864320 | tf_op jit(solution)/shard_map/kaci,kaj->icj/dot_general | solution.py:55
  145.0 0.0 collective-permute-done.3
  145.0 1.0 fusion.135
  146.1 2.6 fusion.8
  148.7 4.3 %fusion.52 = f32[512,2,128]{0,2,1:T(8,128)S(1)} fusion(bf16[8,256,2,512]{3,2,1,0:T(2,128)(2,1)} %param.15, bf16[8,256,512]{2,1,0:T(8,128)(2,1)} %fusion.8, bf16[8,128,512]{2,1,0:T(8,128)(2,1)S(1)} %copy-done), kind=kOutput, calls=%fused_computation.73 | convolution fusion | flops 805568512 | bytes 7864320 | tf_op jit(solution)/shard_map/kaci,kaj->icj/dot_general | solution.py:55
  153.0 93.0 %all-reduce.5 = (bf16[512,2,128]{0,2,1:T(8,128)(2,1)}, bf16[512,2,128]{0,2,1:T(8,128)(2,1)}, bf16[512,2,128]{0,2,1:T(8,128)(2,1)}, bf16[512,2,128]{0,2,1:T(8,128)(2,1)}) all-reduce(f32[512,2,128]{0,2,1:T(8,128)S(1)} %fusion.52, f32[512,2,128]{0,2,1:T(8,128)S(1)} %copy-done.5, ...), channel_id=1, replica_groups=mesh['hist'=4,'rows'=2,'dom'=4] {'hist','rows'}, use_global_device_ids=true, to_apply=%region_10.11 | all-reduce | flops 524288 | bytes 3145728 | tf_op jit(solution)/shard_map/psum | solution.py:58
  246.1 0.0 all-gather.7.cloned.1.call-update
  246.1 0.0 all-gather.5.cloned.1.call-start
  246.1 0.7 all-gather.5.cloned.1.call-update
  246.8 0.0 all-gather.9.cloned.1.call-start
  246.9 0.7 all-gather.9.cloned.1.call-update
  247.6 0.3 all-gather.11.cloned.1.call-start
  247.8 0.6 select_add_fusion.4
  248.5 1.8 select_add_fusion.6
  250.3 0.0 all-gather.11.cloned.1.call-update
  250.3 1.8 select_add_fusion.2
  252.1 1.9 copy.13
  254.0 3.1 copy.11
  257.0 1.8 copy.15
  258.8 0.6 select_add_fusion
  259.5 1.8 copy.17
  261.3 3.9 %multiply_reduce_fusion.2 = f32[1024,2]{0,1:T(2,128)S(1)} fusion(f32[1024,512]{0,1:T(8,128)} %copy.13, bf16[512,2,512]{0,2,1:T(8,128)(2,1)} %all-gather.7.cloned.1.call-done, f32[1024]{0:T(1024)S(1)} %get-tuple-element.47, s32[1024]{0:T(1024)S(1)} %get-tuple-element.53, f32[1024]{0:T(1024)S(1)} %get-tuple-element.46, s32[1024]{0:T(1024)S(1)} %bitcast.138), kind=kOutput, calls=%fused_computation.2 | convolution fusion | flops 1078982656 | bytes 3170304 | tf_op jit(solution)/shard_map/dot_general | solution.py:60
  265.3 13.9 %all-gather.5.cloned.1.call-done = bf16[512,2,512]{0,2,1:T(8,128)(2,1)} async-done(((bf16[512,2,128]{0,2,1:T(8,128)(2,1)}), bf16[512,2,512]{0,2,1:T(8,128)(2,1)}) %all-gather.5.cloned.1.call-update) | async-done | bytes 1048592 | tf_op jit(solution)/shard_map/all_gather | solution.py:59
  279.2 0.0 copy-done.3
  279.2 3.5 %multiply_reduce_fusion.3 = f32[1024,2]{0,1:T(2,128)S(1)} fusion(f32[1024,512]{0,1:T(8,128)S(1)} %copy-done.3, bf16[512,2,512]{0,2,1:T(8,128)(2,1)} %all-gather.5.cloned.1.call-done, f32[1024]{0:T(1024)S(1)} %get-tuple-element.45, s32[1024]{0:T(1024)S(1)} %get-tuple-element.55, f32[1024]{0:T(1024)S(1)} %get-tuple-element.44, s32[1024]{0:T(1024)S(1)} %bitcast.135), kind=kOutput, calls=%fused_computation.3 | convolution fusion | flops 1078982656 | bytes 3170304 | tf_op jit(solution)/shard_map/dot_general | solution.py:60
  282.6 0.0 copy-start.2
  282.6 14.8 %all-gather.9.cloned.1.call-done = bf16[512,2,512]{0,2,1:T(8,128)(2,1)} async-done(((bf16[512,2,128]{0,2,1:T(8,128)(2,1)}), bf16[512,2,512]{0,2,1:T(8,128)(2,1)}) %all-gather.9.cloned.1.call-update) | async-done | bytes 1048592 | tf_op jit(solution)/shard_map/all_gather | solution.py:59
  297.5 3.8 %multiply_reduce_fusion.1 = f32[1024,2]{0,1:T(2,128)S(1)} fusion(f32[1024,512]{0,1:T(8,128)} %copy.15, bf16[512,2,512]{0,2,1:T(8,128)(2,1)} %all-gather.9.cloned.1.call-done, f32[1024]{0:T(1024)S(1)} %get-tuple-element.49, s32[1024]{0:T(1024)S(1)} %get-tuple-element.51, f32[1024]{0:T(1024)S(1)} %get-tuple-element.48, s32[1024]{0:T(1024)S(1)} %bitcast.132), kind=kOutput, calls=%fused_computation.1 | convolution fusion | flops 1078982656 | bytes 3170304 | tf_op jit(solution)/shard_map/dot_general | solution.py:60
  301.3 0.0 copy-start.11
  301.3 14.3 %all-gather.11.cloned.1.call-done = bf16[512,2,512]{0,2,1:T(8,128)(2,1)} async-done(((bf16[512,2,128]{0,2,1:T(8,128)(2,1)}), bf16[512,2,512]{0,2,1:T(8,128)(2,1)}) %all-gather.11.cloned.1.call-update) | async-done | bytes 1048592 | tf_op jit(solution)/shard_map/all_gather | solution.py:59
  315.6 3.5 %multiply_reduce_fusion = f32[1024,2]{0,1:T(2,128)S(1)} fusion(f32[1024,512]{0,1:T(8,128)S(1)} %copy-done.2, bf16[512,2,512]{0,2,1:T(8,128)(2,1)} %all-gather.11.cloned.1.call-done, f32[1024]{0:T(1024)S(1)} %get-tuple-element.11, s32[1024]{0:T(1024)S(1)} %get-tuple-element.57, f32[1024]{0:T(1024)S(1)} %get-tuple-element.10, s32[1024]{0:T(1024)S(1)} %bitcast.129), kind=kOutput, calls=%fused_computation | convolution fusion | flops 1078982656 | bytes 3170304 | tf_op jit(solution)/shard_map/dot_general | solution.py:60
  319.1 0.6 bitcast_add_fusion
  (24 shorter events, 0.1 us)
Async XLA Ops:
  7.2 123.0 %copy-start = (bf16[8,128,512]{2,1,0:T(8,128)(2,1)S(1)}, bf16[8,128,512]{2,1,0:T(8,128)(2,1)}, u32[]{:S(2)}) copy-start(bf16[8,128,512]{2,1,0:T(8,128)(2,1)} %param.14) | copy-start | bytes 3145732
  7.2 17.0 %copy-start.8 = (s32[4,1024]{1,0:T(4,128)S(1)}, s32[4,1024]{1,0:T(4,128)}, u32[]{:S(2)}) copy-start(s32[4,1024]{1,0:T(4,128)} %param.8) | copy-start | bytes 49156
  7.2 17.0 %copy-start.9 = (s32[4,1024]{1,0:T(4,128)S(1)}, s32[4,1024]{1,0:T(4,128)}, u32[]{:S(2)}) copy-start(s32[4,1024]{1,0:T(4,128)} %param.9) | copy-start | bytes 49156
  7.2 17.0 %copy-start.10 = (s32[4,1024]{1,0:T(4,128)S(1)}, s32[4,1024]{1,0:T(4,128)}, u32[]{:S(2)}) copy-start(s32[4,1024]{1,0:T(4,128)} %param.10) | copy-start | bytes 49156
  7.2 17.1 %copy-start.12 = (bf16[1024]{0:T(1024)(128)(2,1)S(1)}, bf16[1024]{0:T(1024)(128)(2,1)}, u32[]{:S(2)}) copy-start(bf16[1024]{0:T(1024)(128)(2,1)} %param.11) | copy-start | bytes 6148
  7.2 254.1 %all-gather.7.cloned.1.call-start = ((), (), s32[]{:S(2)}) async-start(), calls=%async_computation.1 | async-start | bytes 1310720 | tf_op jit(solution)/shard_map/all_gather | solution.py:59
  9.6 117.8 %collective-permute-start = (bf16[256,512]{1,0:T(8,128)(2,1)}, bf16[256,512]{1,0:T(8,128)(2,1)}, u32[]{:S(2)}, u32[]{:S(2)}) collective-permute-start(bf16[256,512]{1,0:T(8,128)(2,1)} %get-tuple-element.28), channel_id=1, source_target_pairs={{0,8},{8,16},{16,24},{1,9},{9,17},{17,25},{2,10},{10,18},{18,26},{... | collective-permute-start | bytes 786440 | tf_op jit(solution)/shard_map/ppermute | solution.py:17
  15.2 113.2 %collective-permute-start.1 = (bf16[256,512]{1,0:T(8,128)(2,1)}, bf16[256,512]{1,0:T(8,128)(2,1)S(1)}, u32[]{:S(2)}, u32[]{:S(2)}) collective-permute-start(bf16[256,512]{1,0:T(8,128)(2,1)} %get-tuple-element.27), channel_id=1, source_target_pairs={{0,8},{8,16},{16,24},{1,9},{9,17},{17,25},{2,10},{10,18},{18,26},{... | collective-permute-start | bytes 786440 | tf_op jit(solution)/shard_map/ppermute | solution.py:17
  18.0 116.5 %collective-permute-start.2 = (bf16[256,512]{1,0:T(8,128)(2,1)}, bf16[256,512]{1,0:T(8,128)(2,1)}, u32[]{:S(2)}, u32[]{:S(2)}) collective-permute-start(bf16[256,512]{1,0:T(8,128)(2,1)} %get-tuple-element.29), channel_id=1, source_target_pairs={{0,8},{8,16},{16,24},{1,9},{9,17},{17,25},{2,10},{10,18},{18,26},{... | collective-permute-start | bytes 786440 | tf_op jit(solution)/shard_map/ppermute | solution.py:17
  22.2 122.8 %collective-permute-start.3 = (bf16[256,512]{1,0:T(8,128)(2,1)}, bf16[256,512]{1,0:T(8,128)(2,1)}, u32[]{:S(2)}, u32[]{:S(2)}) collective-permute-start(bf16[256,512]{1,0:T(8,128)(2,1)} %get-tuple-element.26), channel_id=1, source_target_pairs={{0,8},{8,16},{16,24},{1,9},{9,17},{17,25},{2,10},{10,18},{18,26},{... | collective-permute-start | bytes 786440 | tf_op jit(solution)/shard_map/ppermute | solution.py:17
  128.4 0.7 copy-start.7
  148.7 4.3 %copy-start.4 = (f32[512,2,128]{0,2,1:T(8,128)S(1)}, f32[512,2,128]{0,2,1:T(8,128)}, u32[]{:S(2)}) copy-start(f32[512,2,128]{0,2,1:T(8,128)} %fusion.46) | copy-start | bytes 1572868
  148.7 4.3 %copy-start.5 = (f32[512,2,128]{0,2,1:T(8,128)S(1)}, f32[512,2,128]{0,2,1:T(8,128)}, u32[]{:S(2)}) copy-start(f32[512,2,128]{0,2,1:T(8,128)} %fusion.49) | copy-start | bytes 1572868
  148.7 4.3 %copy-start.6 = (f32[512,2,128]{0,2,1:T(8,128)S(1)}, f32[512,2,128]{0,2,1:T(8,128)}, u32[]{:S(2)}) copy-start(f32[512,2,128]{0,2,1:T(8,128)} %fusion.43) | copy-start | bytes 1572868
  246.1 33.1 %all-gather.5.cloned.1.call-start = ((), (), s32[]{:S(2)}) async-start(), calls=%async_computation | async-start | bytes 1310720 | tf_op jit(solution)/shard_map/all_gather | solution.py:59
  246.8 50.6 %all-gather.9.cloned.1.call-start = ((), (), s32[]{:S(2)}) async-start(), calls=%async_computation.2 | async-start | bytes 1310720 | tf_op jit(solution)/shard_map/all_gather | solution.py:59
  247.6 68.0 %all-gather.11.cloned.1.call-start = ((), (), s32[]{:S(2)}) async-start(), calls=%async_computation.3 | async-start | bytes 1310720 | tf_op jit(solution)/shard_map/all_gather | solution.py:59
  254.0 3.1 copy-start.1
  261.3 17.9 %copy-start.3 = (f32[1024,512]{0,1:T(8,128)S(1)}, f32[1024,512]{0,1:T(8,128)}, u32[]{:S(2)}) copy-start(f32[1024,512]{0,1:T(8,128)} %copy.11) | copy-start | bytes 6291460
  282.6 33.0 %copy-start.2 = (f32[1024,512]{0,1:T(8,128)S(1)}, f32[1024,512]{0,1:T(8,128)}, u32[]{:S(2)}) copy-start(f32[1024,512]{0,1:T(8,128)} %copy.17) | copy-start | bytes 6291460
  301.3 17.8 %copy-start.11 = (f32[2,1024]{1,0:T(2,128)S(1)}, f32[2,1024]{1,0:T(2,128)}, u32[]{:S(2)}) copy-start(f32[2,1024]{1,0:T(2,128)} %param.12) | copy-start | bytes 24580
Sparse Core Ops, SparseCore 0:
  246.2 14.6 all-gather.6
  262.4 16.6 all-gather.4
  280.7 16.6 all-gather.8
  298.9 16.6 all-gather.10
where the time goes:
time: 327 us; the launch traced here: 326 us
  blocking collectives  184 us (56%)
  waiting for transfers between devices  44.5 us (14%)
  matrix products  42.2 us (13%)
  starting transfers between devices  15 us (5%)
  between operations  14.1 us (4%)
  local copies, waits for them, and re-layouts  13.3 us (4%)
  other arithmetic  12.9 us (4%)
    psum x1, blocking collectives, local(): summed = lax.psum(partial_field, ('hist', 'rows')).astype(jnp.bfloat16)  93 us
    psum x1, blocking collectives, local(): whole_grid = lax.psum(partial_grid, ('hist', 'rows', 'dom'))  91.2 us
    all_gather x4, waiting for transfers between devices, local(): field_full = lax.all_gather(summed, 'dom', axis=2, tiled=True)  43.1 us
    dot_general x4, matrix products, local(): jnp.einsum('kaci,kaj->icj', kernel_rows, mixed_rows, preferred_element_ty...  17.5 us
    dot_general x4, matrix products, local(): jnp.dot(row_table, field_full.reshape(NG, 2 * NG), preferred_element_type...  14.7 us
    ppermute x4, starting transfers between devices, from_behind(): return lax.ppermute(array, axis, pairs)  14.6 us
    dot_general x4, matrix products, local(): lax.dot_general(row_charged, col_table, contract_first, preferred_element...  10 us
    add x4, local copies, waits for them, and re-layouts, tables(): lower + jnp.where(places == cell_index[:, None] + 1, fraction[:, None], 0.0)  8.59 us
  transfers between devices with their start and end apart: 8, of which 3 were waited for; matrix products, arithmetic and copies ran while one was open for 16% of the time, Pallas kernels for 0%

commit v1 on v0

v1 whole, which is shorter than its diff:
```python
import functools
import jax
import jax.numpy as jnp
from jax import lax
from jax.experimental import pallas as pl
from jax.experimental.pallas import tpu as pltpu
from jax.sharding import PartitionSpec as P

NG = 512
BINS = 16
STEPS = 4
CORES = 2
PIECES = 8
kick_scale = 0.5

MESH = pl.DeviceIdType.MESH
VM = pl.BlockSpec(memory_space=pltpu.VMEM)
NT = (((1,), (1,)), ((), ()))


def place():
    return lax.axis_index("hist"), lax.axis_index("rows"), lax.axis_index("dom")


def hat(first, extent, where):
    places = lax.broadcasted_iota(jnp.int32, (extent, where.shape[1]), 0) + first
    gap = (places.astype(jnp.float32) - where).astype(jnp.bfloat16)
    return jnp.maximum(jnp.bfloat16(1.0) - jnp.abs(gap), jnp.bfloat16(0.0))


def plane_peer(rows, dom, shift):
    h, r, d = place()
    other = lax.rem(r * dom + d + shift, rows * dom)
    return other, (h, other // dom, lax.rem(other, dom))


def plane_barrier(rows, dom):
    barrier = pltpu.get_barrier_semaphore()
    for shift in range(1, rows * dom):
        pl.semaphore_signal(barrier, inc=1, device_id=plane_peer(rows, dom, shift)[1], device_id_type=MESH)
    pl.semaphore_wait(barrier, rows * dom - 1)


def gather_kernel(rows, dom, row_ref, col_ref, bin_ref, charge_ref, spots, out, charges, total,
                  send, recv, send_c, recv_c):
    _, r, d = place()
    n = rows * dom
    _, band, width = out.shape
    bins = bin_ref[...]
    row_bin = bins // BINS
    spots[0, 0:STEPS] = row_ref[...].astype(jnp.float32) + (row_bin.astype(jnp.float32) + 0.5) / BINS
    spots[0, STEPS:] = col_ref[...].astype(jnp.float32) + ((bins - row_bin * BINS).astype(jnp.float32) + 0.5) / BINS
    charges[0] = charge_ref[...]
    plane_barrier(rows, dom)

    def pair(shift):
        _, device = plane_peer(rows, dom, shift)
        return (
            pltpu.make_async_remote_copy(
                src_ref=spots.at[0], dst_ref=spots.at[shift], send_sem=send.at[shift], recv_sem=recv.at[shift],
                device_id=device, device_id_type=MESH),
            pltpu.make_async_remote_copy(
                src_ref=charge_ref, dst_ref=charges.at[shift], send_sem=send_c.at[shift],
                recv_sem=recv_c.at[shift], device_id=device, device_id_type=MESH))

    for shift in range(1, n):
        for copy in pair(shift):
            copy.start()
    total[...] = jnp.zeros_like(total)

    def add(shift):
        charge = charges[shift].astype(jnp.bfloat16)
        for s in range(STEPS):
            row = hat(r * band, band, spots[shift, s:s + 1, :]) * charge
            col = hat(d * width, width, spots[shift, STEPS + s:STEPS + s + 1, :])
            total[STEPS - 1 - s] += lax.dot_general(row, col, NT, preferred_element_type=jnp.float32)

    add(0)

    def step(shift, carry):
        for copy in pair(shift):
            copy.wait_recv()
        add(shift)
        return carry

    lax.fori_loop(1, n, step, 0)
    out[...] = total[...].astype(out.dtype)
    for shift in range(1, n):
        for copy in pair(shift):
            copy.wait_send()


def deposit(row_index, col_index, bin_index, charge, rows, dom, band, width):
    n = rows * dom
    own = row_index.shape[1]
    tile = (STEPS, band, width)
    return pl.pallas_call(
        functools.partial(gather_kernel, rows, dom),
        out_shape=(jax.ShapeDtypeStruct((n, 2 * STEPS, own), jnp.float32),
                   jax.ShapeDtypeStruct(tile, jnp.bfloat16)),
        in_specs=[VM] * 4, out_specs=(VM, VM),
        scratch_shapes=[pltpu.VMEM((n, 1, own), charge.dtype), pltpu.VMEM(tile, jnp.float32)]
        + [pltpu.SemaphoreType.DMA((n,))] * 4,
        compiler_params=pltpu.CompilerParams(collective_id=1, has_side_effects=True),
    )(row_index, col_index, bin_index, charge)


def shift_kernel(hist, rows, dom, part, tail, out, arrived, summed,
                 sem_hs, sem_hr, sem_cs, sem_cr, sem_xs, sem_xr, sem_ps, sem_pr, sem_fs, sem_fr):
    h, r, d = place()
    chips = dom // CORES
    up, down = (h + 1, r, d), (h - 1, r, d)
    partner = (h, r, d + 1 - 2 * lax.rem(d, CORES))
    is_first, is_last = h == 0, h == hist - 1
    barrier = pltpu.get_barrier_semaphore()

    @pl.when(jnp.logical_not(is_last))
    def _():
        pl.semaphore_signal(barrier, inc=1, device_id=up, device_id_type=MESH)

    @pl.when(jnp.logical_not(is_first))
    def _():
        pl.semaphore_signal(barrier, inc=1, device_id=down, device_id_type=MESH)

    across = [(h, r, lax.rem(d + CORES * j, dom)) for j in range(1, chips)]
    pl.semaphore_signal(barrier, inc=1, device_id=partner, device_id_type=MESH)
    for device in across:
        pl.semaphore_signal(barrier, inc=1, device_id=device, device_id_type=MESH)
    count = chips + jnp.where(is_first, 0, 1) + jnp.where(is_last, 0, 1)
    pl.semaphore_wait(barrier, count)

    def remote(src, dst, s_sem, r_sem, device):
        return pltpu.make_async_remote_copy(src_ref=src, dst_ref=dst, send_sem=s_sem, recv_sem=r_sem,
                                            device_id=device, device_id_type=MESH)

    def tail_copy(c):
        width = part.shape[2]
        columns = pl.ds(pl.multiple_of(d * width, width), width)
        return remote(tail.at[tail.shape[0] - STEPS + c, :, columns], out.at[d, c], sem_hs.at[c], sem_hr.at[c], up)

    def chain_copy(src, c):
        return remote(src.at[c], arrived.at[c], sem_cs.at[c], sem_cr.at[c], down)

    def cross_copy(c, j):
        return remote(out.at[d, c], out.at[d, c], sem_xs.at[c, j], sem_xr.at[c, j], across[j - 1])

    def partner_copy(c):
        return remote(out.at[d, c], out.at[d, c], sem_ps.at[c], sem_pr.at[c], partner)

    def forward_copy(c, j):
        other = lax.rem(d + CORES * (chips - j), dom)
        return remote(out.at[other, c], out.at[other, c], sem_fs.at[c, j], sem_fr.at[c, j], partner)

    @pl.when(is_last)
    def _():
        for c in range(STEPS):
            chain_copy(part, c).start()

    @pl.when(jnp.logical_not(is_last))
    def _():
        for c in range(STEPS):
            tail_copy(c).start()

    for c in range(STEPS):
        @pl.when(jnp.logical_not(is_last))
        def _():
            chain_copy(part, c).wait_recv()
            both = part[c].astype(jnp.float32) + arrived[c].astype(jnp.float32)

            @pl.when(is_first)
            def _():
                out[d, c] = both.astype(out.dtype)

            @pl.when(jnp.logical_not(is_first))
            def _():
                summed[c] = both.astype(out.dtype)
                chain_copy(summed, c).start()

        @pl.when(jnp.logical_not(is_first))
        def _():
            tail_copy(c).wait_recv()

        for j in range(1, chips):
            cross_copy(c, j).start()
        partner_copy(c).start()
    for c in range(STEPS):
        for j in range(1, chips):
            cross_copy(c, j).wait_recv()
            forward_copy(c, j).start()
    for c in range(STEPS):
        partner_copy(c).wait()
        for j in range(1, chips):
            forward_copy(c, j).wait()
            cross_copy(c, j).wait_send()

    @pl.when(jnp.logical_not(is_first))
    def _():
        for c in range(STEPS):
            chain_copy(part, c).wait_send()

    @pl.when(jnp.logical_not(is_last))
    def _():
        for c in range(STEPS):
            tail_copy(c).wait_send()


def newest_grids(part, tail, hist, rows, dom):
    chips = dom // CORES
    dma = pltpu.SemaphoreType.DMA
    return pl.pallas_call(
        functools.partial(shift_kernel, hist, rows, dom),
        out_shape=jax.ShapeDtypeStruct((dom,) + part.shape, part.dtype),
        in_specs=[VM, pl.BlockSpec(memory_space=pl.ANY)], out_specs=VM,
        scratch_shapes=[pltpu.VMEM(part.shape, part.dtype)] * 2
        + [dma((STEPS,))] * 4 + [dma((STEPS, chips))] * 2 + [dma((STEPS,))] * 2 + [dma((STEPS, chips))] * 2,
        compiler_params=pltpu.CompilerParams(collective_id=2, has_side_effects=True),
    )(part, tail)


def field_kernel(rows, new_ref, old_ref, cols_ref, rows_ref, out, own_out, cycle_out, grids, total):
    k = pl.program_id(0)
    lags = pl.num_programs(0)
    dom, _, band, width = new_ref.shape
    count = old_ref.shape[0]
    piece = NG // rows

    @pl.when(k == 0)
    def _():
        for d in range(dom):
            grids[0:STEPS, :, d * width:(d + 1) * width] = new_ref[d]
        grids[STEPS:] = old_ref[...]
        cycle_out[...] = grids[0:count]
        total[...] = jnp.zeros_like(total)

    window = grids[pl.ds(k, STEPS)].reshape(STEPS * band, NG)
    mixed = lax.dot_general(cols_ref[0], window, NT, preferred_element_type=jnp.float32).astype(jnp.bfloat16)
    stacked = jnp.concatenate(
        [mixed[:, (STEPS - 1 - s) * band:(STEPS - s) * band] for s in range(STEPS)], axis=0)
    for comp in range(2):
        total[comp] += jnp.dot(stacked, rows_ref[0, comp], preferred_element_type=jnp.float32)

    @pl.when(k == lags - 1)
    def _():
        for r in range(rows):
            block = jnp.concatenate([total[comp, :, r * piece:(r + 1) * piece] for comp in range(2)], axis=1)
            out[r] = block.astype(out.dtype)

            @pl.when(lax.axis_index("rows") == r)
            def _():
                own_out[...] = block


def field_parts(new, old, kernel_cols, rows_t, rows):
    lags, width, _ = kernel_cols.shape
    band = old.shape[1]
    return pl.pallas_call(
        functools.partial(field_kernel, rows),
        grid=(lags,),
        out_shape=(jax.ShapeDtypeStruct((rows, STEPS * width, 2 * NG // rows), jnp.bfloat16),
                   jax.ShapeDtypeStruct((STEPS * width, 2 * NG // rows), jnp.float32),
                   jax.ShapeDtypeStruct(old.shape, old.dtype)),
        in_specs=[pl.BlockSpec(new.shape, lambda k: (0, 0, 0, 0)),
                  pl.BlockSpec(old.shape, lambda k: (0, 0, 0)),
                  pl.BlockSpec((1, width, NG), lambda k: (k, 0, 0)),
                  pl.BlockSpec((1, 2, band, NG), lambda k: (k, 0, 0, 0))],
        out_specs=(pl.BlockSpec((rows, STEPS * width, 2 * NG // rows), lambda k: (0, 0, 0)),
                   pl.BlockSpec((STEPS * width, 2 * NG // rows), lambda k: (0, 0)),
                   pl.BlockSpec(old.shape, lambda k: (0, 0, 0))),
        scratch_shapes=[pltpu.VMEM((lags + STEPS, band, NG), old.dtype),
                        pltpu.VMEM((2, STEPS * width, NG), jnp.float32)],
    )(new, old, kernel_cols, rows_t)


def sum_kernel(hist, rows, dom, parts, own, spots, momentum, out, got, mine, from_low, from_high, to_high, to_low,
               kicks, got_kicks, sem_ys, sem_yr, sem_us, sem_ur, sem_ds, sem_dr, sem_ks, sem_kr):
    h, r, d = place()
    n = rows * dom
    tall, wide = own.shape
    width, band = tall // STEPS, wide // 2
    size = tall // PIECES
    kind = parts.dtype
    up, down = (h + 1, r, d), (h - 1, r, d)
    is_first, is_last = h == 0, h == hist - 1
    inner = jnp.logical_and(h > 0, h < hist - 1)
    barrier = pltpu.get_barrier_semaphore()

    @pl.when(jnp.logical_not(is_last))
    def _():
        pl.semaphore_signal(barrier, inc=1, device_id=up, device_id_type=MESH)

    @pl.when(jnp.logical_not(is_first))
    def _():
        pl.semaphore_signal(barrier, inc=1, device_id=down, device_id_type=MESH)

    for shift in range(1, n):
        pl.semaphore_signal(barrier, inc=1, device_id=plane_peer(rows, dom, shift)[1], device_id_type=MESH)
    pl.semaphore_wait(barrier, n - 1 + jnp.where(is_first, 0, 1) + jnp.where(is_last, 0, 1))

    def span(c):
        return pl.ds(pl.multiple_of(c * size, size), size)

    def row_copy(c, j):
        other = lax.rem(r + j, rows)
        return pltpu.make_async_remote_copy(
            src_ref=parts.at[other, span(c)], dst_ref=got.at[j, span(c)], send_sem=sem_ys.at[c, j],
            recv_sem=sem_yr.at[c, j], device_id=(h, other, d), device_id_type=MESH)

    def up_copy(c):
        return pltpu.make_async_remote_copy(
            src_ref=to_high.at[span(c)], dst_ref=from_low.at[span(c)], send_sem=sem_us.at[c],
            recv_sem=sem_ur.at[c], device_id=up, device_id_type=MESH)

    def down_copy(c):
        return pltpu.make_async_remote_copy(
            src_ref=to_low.at[span(c)], dst_ref=from_high.at[span(c)], send_sem=sem_ds.at[c],
            recv_sem=sem_dr.at[c], device_id=down, device_id_type=MESH)

    for c in range(PIECES):
        for j in range(1, rows):
            row_copy(c, j).start()

    kicks[...] = jnp.zeros_like(kicks)

    def kick(s):
        rows_s = pl.ds(pl.multiple_of(s * width, width), width)
        value = mine[rows_s]
        stacked = jnp.concatenate([value[:, :band], value[:, band:]], axis=0)
        coarse = stacked.astype(kind)
        fine = (stacked - coarse.astype(jnp.float32)).astype(kind)
        table = jnp.concatenate([coarse, fine], axis=0)

        def block(k, carry):
            row = hat(r * band, band, spots[k, pl.ds(s, 1), :])
            col = hat(d * width, width, spots[k, pl.ds(STEPS + s, 1), :]).astype(jnp.float32)
            along = jnp.dot(table, row, preferred_element_type=jnp.float32)
            for comp in range(2):
                both = (along[comp * width:(comp + 1) * width]
                        + along[(2 + comp) * width:(3 + comp) * width])
                kicks[k, comp:comp + 1, :] += jnp.sum(both * col, axis=0, keepdims=True)
            return carry

        lax.fori_loop(0, n, block, 0)

    lag = 2 * (hist - 2)
    group = PIECES // STEPS

    def step(t, carry):
        @pl.when(t < PIECES)
        def _():
            value = own[span(t)]
            for j in range(1, rows):
                row_copy(t, j).wait_recv()
                value += got[j, span(t)].astype(jnp.float32)
            mine[span(t)] = value

            @pl.when(is_first)
            def _():
                to_high[span(t)] = value.astype(kind)
                up_copy(t).start()

            @pl.when(is_last)
            def _():
                to_low[span(t)] = value.astype(kind)
                down_copy(t).start()

        low = t - 2 * h

        @pl.when(jnp.logical_and(inner, jnp.logical_and(low >= 0, low < PIECES)))
        def _():
            up_copy(low).wait_recv()
            to_high[span(low)] = (mine[span(low)] + from_low[span(low)].astype(jnp.float32)).astype(kind)
            up_copy(low).start()

        high = t - 2 * (hist - 1 - h)

        @pl.when(jnp.logical_and(inner, jnp.logical_and(high >= 0, high < PIECES)))
        def _():
            down_copy(high).wait_recv()
            to_low[span(high)] = (mine[span(high)] + from_high[span(high)].astype(jnp.float32)).astype(kind)
            down_copy(high).start()

        done = t - lag

        @pl.when(done >= 0)
        def _():
            @pl.when(is_first)
            def _():
                down_copy(done).wait_recv()
                mine[span(done)] = mine[span(done)] + from_high[span(done)].astype(jnp.float32)

            @pl.when(is_last)
            def _():
                up_copy(done).wait_recv()
                mine[span(done)] = mine[span(done)] + from_low[span(done)].astype(jnp.float32)

            @pl.when(inner)
            def _():
                mine[span(done)] = (mine[span(done)] + from_low[span(done)].astype(jnp.float32)
                                    + from_high[span(done)].astype(jnp.float32))

            @pl.when(lax.rem(done, group) == group - 1)
            def _():
                kick(done // group)

        return carry

    lax.fori_loop(0, PIECES + lag, step, 0)

    def kick_copy(k):
        _, device = plane_peer(rows, dom, n - k)
        return pltpu.make_async_remote_copy(
            src_ref=kicks.at[k], dst_ref=got_kicks.at[k], send_sem=sem_ks.at[k], recv_sem=sem_kr.at[k],
            device_id=device, device_id_type=MESH)

    for k in range(1, n):
        kick_copy(k).start()

    def finish(c, carry):
        @pl.when(jnp.logical_not(is_last))
        def _():
            up_copy(c).wait_send()

        @pl.when(jnp.logical_not(is_first))
        def _():
            down_copy(c).wait_send()

        for j in range(1, rows):
            row_copy(c, j).wait_send()
        return carry

    lax.fori_loop(0, PIECES, finish, 0)
    total = kicks[0]
    for k in range(1, n):
        kick_copy(k).wait()
        total = total + got_kicks[k]
    out[...] = momentum[...] + kick_scale * total


def sum_and_kick(parts, own, spots, momentum, hist, rows, dom):
    tall, wide = own.shape
    n = rows * dom
    dma = pltpu.SemaphoreType.DMA
    flat = pltpu.VMEM((tall, wide), parts.dtype)
    each = pltpu.VMEM((n,) + momentum.shape, momentum.dtype)
    return pl.pallas_call(
        functools.partial(sum_kernel, hist, rows, dom),
        out_shape=jax.ShapeDtypeStruct(momentum.shape, momentum.dtype),
        in_specs=[VM] * 4, out_specs=VM,
        scratch_shapes=[pltpu.VMEM(parts.shape, parts.dtype), pltpu.VMEM((tall, wide), jnp.float32),
                        flat, flat, flat, flat, each, each]
        + [dma((PIECES, rows))] * 2 + [dma((PIECES,))] * 4 + [dma((n,))] * 2,
        compiler_params=pltpu.CompilerParams(collective_id=3, has_side_effects=True),
    )(parts, own, spots, momentum)


def local(hist, rows, dom, row_index, col_index, bin_index, charge, momentum, history, kernel_cols, kernel_rows):
    band = history.shape[1]
    width = kernel_cols.shape[1]
    spots, part = deposit(row_index, col_index, bin_index, charge.astype(jnp.float32)[None], rows, dom, band, width)
    new = newest_grids(part, history, hist, rows, dom)
    rows_t = jnp.transpose(kernel_rows, (0, 2, 1, 3))
    parts, own, cycle_now = field_parts(new, history, kernel_cols, rows_t, rows)
    return sum_and_kick(parts, own, spots, momentum, hist, rows, dom), cycle_now


def solution(mesh):
    spread = ("hist", "rows", "dom")
    in_specs = (P(None, spread), P(None, spread), P(None, spread), P(spread), P(None, spread),
                P("hist", "rows", None), P("hist", "dom", None), P("hist", "rows", None, None))
    out_specs = (P(None, spread), P("hist", "rows", None))
    sizes = mesh.shape
    body = functools.partial(local, sizes["hist"], sizes["rows"], sizes["dom"])
    return jax.shard_map(body, mesh=mesh, in_specs=in_specs, out_specs=out_specs, check_vma=False)
```

time: 327 us -> 102 us (0.31)
  blocking collectives: 184 us -> 0 us
  Pallas kernels: 0 us -> 93.3 us
  waiting for transfers between devices: 44.5 us -> 0 us
  matrix products: 42.2 us -> 0 us
  starting transfers between devices: 15 us -> 0 us
  between operations: 14.1 us -> 0.65 us
  other arithmetic: 12.9 us -> 1.28 us
  local copies, waits for them, and re-layouts: 13.3 us -> 6.27 us
    psum x2 -> x0, blocking collectives: 184 us -> none  [the longest x1 93 us: local(): summed = lax.psum(partial_field, ('hist', 'rows')).astype(jnp.bfloat16)]
    pallas_call x0 -> x4, Pallas kernels: none -> 93.3 us  [the longest x1 43 us: sum_and_kick(): pl.pallas_call(functools.partial(sum_kernel, hist, rows, dom), out_shape=...]
    all_gather x4 -> x0, waiting for transfers between devices: 43.1 us -> none  [local(): field_full = lax.all_gather(summed, 'dom', axis=2, tiled=True)]
    dot_general x12 -> x0, matrix products: 42.2 us -> none  [the longest x4 17.5 us: local(): jnp.einsum('kaci,kaj->icj', kernel_rows, mixed_rows, preferred_element_ty...]
    ppermute x4 -> x0, starting transfers between devices: 14.6 us -> none  [from_behind(): return lax.ppermute(array, axis, pairs)]
    add x4 -> x0, local copies, waits for them, and re-layouts: 8.59 us -> none  [tables(): lower + jnp.where(places == cell_index[:, None] + 1, fraction[:, None], 0.0)]
    unnamed x26 -> x2, local copies, waits for them, and re-layouts: 0.75 us -> 6.27 us
    add x9 -> x0, other arithmetic: 5.45 us -> none  [the longest x4 4.82 us: tables(): lower + jnp.where(places == cell_index[:, None] + 1, fraction[:, None], 0.0)]
  transfers between devices with their start and end apart: 8 -> 0, of which waited for: 3 -> 0; matrix products, arithmetic and copies ran while one was open for 16% -> 0% of each run, Pallas kernels for 0% -> 0%
where the time goes in v1:
time: 102 us; the launch traced here: 101 us
  Pallas kernels  93.3 us (91%)
  local copies, waits for them, and re-layouts  6.27 us (6%)
  other arithmetic  1.28 us (1%)
    pallas_call x1, Pallas kernels, sum_and_kick(): pl.pallas_call(functools.partial(sum_kernel, hist, rows, dom), out_shape=...  43 us
    pallas_call x1, Pallas kernels, newest_grids(): pl.pallas_call(functools.partial(shift_kernel, hist, rows, dom), out_shap...  23.6 us
    pallas_call x1, Pallas kernels, deposit(): pl.pallas_call(functools.partial(gather_kernel, rows, dom), out_shape=(ja...  14.2 us
    pallas_call x1, Pallas kernels, field_parts(): pl.pallas_call(functools.partial(field_kernel, rows), grid=(lags,), out_s...  12.6 us
    unnamed x2, local copies, waits for them, and re-layouts  6.27 us

profile of v1, /device:TPU:0, one launch (start us, length us, event | category | flops | bytes accessed | tf_op | source)
XLA Modules:
  0.0 101.5 jit_solution(10474195622349082001)
XLA Ops:
  0.6 1.3 %broadcast_in_dim.7 = f32[1024]{0:T(1024)} convert(bf16[1024]{0:T(1024)(128)(2,1)} %param.11) | non-fusion elementwise | flops 1024 | bytes 6144 | tf_op jit(solution)/shard_map/broadcast_in_dim | solution.py:459
  1.9 14.2 %shard_map.95 = (f32[8,8,1024]{2,1,0:T(8,128)}, bf16[4,256,128]{2,1,0:T(8,128)(2,1)}) custom-call(s32[4,1024]{1,0:T(4,128)} %row_ref.1, s32[4,1024]{1,0:T(4,128)} %col_ref.1, s32[4,1024]{1,0:T(4,128)} %bin_ref.1, f32[1,1024]{1,0:T(1,128)} %bitcast.5), custom_call_target="tpu_custom_call" | custom-call | tf_op jit(solution)/shard_map/pallas_call | solution.py:97
  16.1 23.6 %shard_map.96.new_ref = bf16[4,4,256,128]{3,2,1,0:T(8,128)(2,1)} custom-call(bf16[4,256,128]{2,1,0:T(8,128)(2,1)} %get-tuple-element.7.part, bf16[8,256,512]{2,1,0:T(8,128)(2,1)} %old_ref.1), custom_call_target="tpu_custom_call" | custom-call | tf_op jit(solution)/shard_map/pallas_call | solution.py:210
  39.6 5.0 %copy.12 = bf16[8,256,2,512]{3,1,2,0:T(8,128)(2,1)} copy(bf16[8,256,2,512]{3,2,1,0:T(2,128)(2,1)} %param.15) | data formatting | bytes 8388608 | tf_op args[7]
  44.6 12.6 %shard_map.97 = (bf16[2,512,512]{2,1,0:T(8,128)(2,1)}, f32[512,512]{1,0:T(8,128)}, bf16[8,256,512]{2,1,0:T(8,128)(2,1)}) custom-call(bf16[4,4,256,128]{3,2,1,0:T(8,128)(2,1)} %shard_map.96.new_ref, bf16[8,256,512]{2,1,0:T(8,128)(2,1)} %old_ref.1, bf16[8,128,512]{2,1,0:T(8,128)(2,1)} %cols_ref.1, bf16[8,2,256,512]{3,2,1,0:T(8,128)(2,1)} %bitcast.4), custom_call_target="tpu_custom_call" | custom-call | tf_op jit(solution)/shard_map/pallas_call | solution.py:256
  57.2 43.0 %shard_map.98 = f32[2,1024]{1,0:T(2,128)} custom-call(bf16[2,512,512]{2,1,0:T(8,128)(2,1)} %get-tuple-element.8.parts, f32[512,512]{1,0:T(8,128)} %get-tuple-element.9.own, f32[8,8,1024]{2,1,0:T(8,128)} %get-tuple-element.10.spots, f32[2,1024]{1,0:T(2,128)} %momentum.1), custom_call_target="tpu_custom_call" | custom-call | tf_op jit(solution)/shard_map/pallas_call | solution.py:445
  100.2 1.3 %copy.14 = f32[2,1024]{1,0:T(2,128)} copy(f32[2,1024]{1,0:T(2,128)} %shard_map.98) | data formatting | bytes 16384

commit v2 on v1

--- a/solution.py
+++ b/solution.py
@@ -105,8 +105,17 @@
     )(row_index, col_index, bin_index, charge)
 
 
-def shift_kernel(hist, rows, dom, part, tail, out, arrived, summed,
+def field_kernel(hist, rows, dom, part, old_ref, cols_ref, rows_ref, parts, own_out, newest,
+                 out, arrived, summed, grids, cols, rows_in, total, load,
                  sem_hs, sem_hr, sem_cs, sem_cr, sem_xs, sem_xr, sem_ps, sem_pr, sem_fs, sem_fr):
+    lags, width, _ = cols.shape
+    band = part.shape[1]
+    piece = NG // rows
+    loads = (pltpu.make_async_copy(old_ref, grids.at[pl.ds(STEPS, lags)], load.at[0]),
+             pltpu.make_async_copy(cols_ref, cols, load.at[1]),
+             pltpu.make_async_copy(rows_ref, rows_in, load.at[2]))
+    for copy in loads:
+        copy.start()
     h, r, d = place()
     chips = dom // CORES
     up, down = (h + 1, r, d), (h - 1, r, d)
@@ -134,9 +143,8 @@
                                             device_id=device, device_id_type=MESH)
 
     def tail_copy(c):
-        width = part.shape[2]
         columns = pl.ds(pl.multiple_of(d * width, width), width)
-        return remote(tail.at[tail.shape[0] - STEPS + c, :, columns], out.at[d, c], sem_hs.at[c], sem_hr.at[c], up)
+        return remote(old_ref.at[lags - STEPS + c, :, columns], out.at[d, c], sem_hs.at[c], sem_hr.at[c], up)
 
     def chain_copy(src, c):
         return remote(src.at[c], arrived.at[c], sem_cs.at[c], sem_cr.at[c], down)
@@ -161,36 +169,91 @@
         for c in range(STEPS):
             tail_copy(c).start()
 
+    def products(k, first, steps):
+        window = grids[pl.ds(k + STEPS - first - steps, steps)].reshape(steps * band, NG)
+        mixed = lax.dot_general(cols[k], window, NT, preferred_element_type=jnp.float32).astype(part.dtype)
+        stacked = jnp.concatenate(
+            [mixed[:, (steps - 1 - s) * band:(steps - s) * band] for s in range(steps)], axis=0)
+        span = slice(first * width, (first + steps) * width)
+        for comp in range(2):
+            total[comp, span] += jnp.dot(stacked, rows_in[k, comp], preferred_element_type=jnp.float32)
+
+    def travel():
+        for c in range(STEPS):
+            @pl.when(jnp.logical_not(is_last))
+            def _():
+                chain_copy(part, c).wait_recv()
+                both = part[c].astype(jnp.float32) + arrived[c].astype(jnp.float32)
+
+                @pl.when(is_first)
+                def _():
+                    out[d, c] = both.astype(out.dtype)
+
+                @pl.when(jnp.logical_not(is_first))
+                def _():
+                    summed[c] = both.astype(out.dtype)
+                    chain_copy(summed, c).start()
+
+            @pl.when(jnp.logical_not(is_first))
+            def _():
+                tail_copy(c).wait_recv()
+
+            for j in range(1, chips):
+                cross_copy(c, j).start()
+            partner_copy(c).start()
+        for c in range(STEPS):
+            for j in range(1, chips):
+                cross_copy(c, j).wait_recv()
+                forward_copy(c, j).start()
+
+    def compute():
+        total[...] = jnp.zeros_like(total)
+        for copy in loads:
+            copy.wait()
+
+        def lag(k, carry):
+            products(k, 0, STEPS)
+            return carry
+
+        lax.fori_loop(STEPS, lags, lag, 0)
+        for k in range(1, STEPS):
+            products(k, 0, k)
+
+    def phase(turn, carry):
+        now = jnp.logical_xor(turn == 0, is_first)
+
+        @pl.when(now)
+        def _():
+            travel()
+
+        @pl.when(jnp.logical_not(now))
+        def _():
+            compute()
+
+        return carry
+
+    lax.fori_loop(0, 2, phase, 0)
     for c in range(STEPS):
-        @pl.when(jnp.logical_not(is_last))
-        def _():
-            chain_copy(part, c).wait_recv()
-            both = part[c].astype(jnp.float32) + arrived[c].astype(jnp.float32)
-
-            @pl.when(is_first)
-            def _():
-                out[d, c] = both.astype(out.dtype)
-
-            @pl.when(jnp.logical_not(is_first))
-            def _():
-                summed[c] = both.astype(out.dtype)
-                chain_copy(summed, c).start()
-
-        @pl.when(jnp.logical_not(is_first))
-        def _():
-            tail_copy(c).wait_recv()
-
+        partner_copy(c).wait_recv()
         for j in range(1, chips):
-            cross_copy(c, j).start()
-        partner_copy(c).start()
+            forward_copy(c, j).wait_recv()
+    for e in range(dom):
+        grids[0:STEPS, :, e * width:(e + 1) * width] = out[e]
+    newest[...] = grids[0:STEPS]
+    for k in range(STEPS):
+        products(k, k, STEPS - k)
+    for q in range(rows):
+        block = jnp.concatenate([total[comp, :, q * piece:(q + 1) * piece] for comp in range(2)], axis=1)
+        parts[q] = block.astype(parts.dtype)
+
+        @pl.when(r == q)
+        def _():
+            own_out[...] = block
+
     for c in range(STEPS):
+        partner_copy(c).wait_send()
         for j in range(1, chips):
-            cross_copy(c, j).wait_recv()
-            forward_copy(c, j).start()
-    for c in range(STEPS):
-        partner_copy(c).wait()
-        for j in range(1, chips):
-            forward_copy(c, j).wait()
+            forward_copy(c, j).wait_send()
             cross_copy(c, j).wait_send()
 
     @pl.when(jnp.logical_not(is_first))
@@ -204,71 +267,28 @@
             tail_copy(c).wait_send()
 
 
-def newest_grids(part, tail, hist, rows, dom):
+def field_parts(part, old, kernel_cols, rows_t, hist, rows, dom):
+    lags, width, _ = kernel_cols.shape
+    band = old.shape[1]
     chips = dom // CORES
     dma = pltpu.SemaphoreType.DMA
+    anywhere = pl.BlockSpec(memory_space=pl.ANY)
+    wide = (STEPS * width, 2 * NG // rows)
     return pl.pallas_call(
-        functools.partial(shift_kernel, hist, rows, dom),
-        out_shape=jax.ShapeDtypeStruct((dom,) + part.shape, part.dtype),
-        in_specs=[VM, pl.BlockSpec(memory_space=pl.ANY)], out_specs=VM,
-        scratch_shapes=[pltpu.VMEM(part.shape, part.dtype)] * 2
+        functools.partial(field_kernel, hist, rows, dom),
+        out_shape=(jax.ShapeDtypeStruct((rows,) + wide, jnp.bfloat16),
+                   jax.ShapeDtypeStruct(wide, jnp.float32),
+                   jax.ShapeDtypeStruct((STEPS, band, NG), old.dtype)),
+        in_specs=[VM, anywhere, anywhere, anywhere], out_specs=(VM, VM, VM),
+        scratch_shapes=[pltpu.VMEM((dom,) + part.shape, part.dtype), pltpu.VMEM(part.shape, part.dtype),
+                        pltpu.VMEM(part.shape, part.dtype),
+                        pltpu.VMEM((lags + STEPS, band, NG), old.dtype),
+                        pltpu.VMEM(kernel_cols.shape, kernel_cols.dtype),
+                        pltpu.VMEM(rows_t.shape, rows_t.dtype),
+                        pltpu.VMEM((2, STEPS * width, NG), jnp.float32), dma((3,))]
         + [dma((STEPS,))] * 4 + [dma((STEPS, chips))] * 2 + [dma((STEPS,))] * 2 + [dma((STEPS, chips))] * 2,
         compiler_params=pltpu.CompilerParams(collective_id=2, has_side_effects=True),
-    )(part, tail)
-
-
-def field_kernel(rows, new_ref, old_ref, cols_ref, rows_ref, out, own_out, cycle_out, grids, total):
-    k = pl.program_id(0)
-    lags = pl.num_programs(0)
-    dom, _, band, width = new_ref.shape
-    count = old_ref.shape[0]
-    piece = NG // rows
-
-    @pl.when(k == 0)
-    def _():
-        for d in range(dom):
-            grids[0:STEPS, :, d * width:(d + 1) * width] = new_ref[d]
-        grids[STEPS:] = old_ref[...]
-        cycle_out[...] = grids[0:count]
-        total[...] = jnp.zeros_like(total)
-
-    window = grids[pl.ds(k, STEPS)].reshape(STEPS * band, NG)
-    mixed = lax.dot_general(cols_ref[0], window, NT, preferred_element_type=jnp.float32).astype(jnp.bfloat16)
-    stacked = jnp.concatenate(
-        [mixed[:, (STEPS - 1 - s) * band:(STEPS - s) * band] for s in range(STEPS)], axis=0)
-    for comp in range(2):
-        total[comp] += jnp.dot(stacked, rows_ref[0, comp], preferred_element_type=jnp.float32)
-
-    @pl.when(k == lags - 1)
-    def _():
-        for r in range(rows):
-            block = jnp.concatenate([total[comp, :, r * piece:(r + 1) * piece] for comp in range(2)], axis=1)
-            out[r] = block.astype(out.dtype)
-
-            @pl.when(lax.axis_index("rows") == r)
-            def _():
-                own_out[...] = block
-
-
-def field_parts(new, old, kernel_cols, rows_t, rows):
-    lags, width, _ = kernel_cols.shape
-    band = old.shape[1]
-    return pl.pallas_call(
-        functools.partial(field_kernel, rows),
-        grid=(lags,),
-        out_shape=(jax.ShapeDtypeStruct((rows, STEPS * width, 2 * NG // rows), jnp.bfloat16),
-                   jax.ShapeDtypeStruct((STEPS * width, 2 * NG // rows), jnp.float32),
-                   jax.ShapeDtypeStruct(old.shape, old.dtype)),
-        in_specs=[pl.BlockSpec(new.shape, lambda k: (0, 0, 0, 0)),
-                  pl.BlockSpec(old.shape, lambda k: (0, 0, 0)),
-                  pl.BlockSpec((1, width, NG), lambda k: (k, 0, 0)),
-                  pl.BlockSpec((1, 2, band, NG), lambda k: (k, 0, 0, 0))],
-        out_specs=(pl.BlockSpec((rows, STEPS * width, 2 * NG // rows), lambda k: (0, 0, 0)),
-                   pl.BlockSpec((STEPS * width, 2 * NG // rows), lambda k: (0, 0)),
-                   pl.BlockSpec(old.shape, lambda k: (0, 0, 0))),
-        scratch_shapes=[pltpu.VMEM((lags + STEPS, band, NG), old.dtype),
-                        pltpu.VMEM((2, STEPS * width, NG), jnp.float32)],
-    )(new, old, kernel_cols, rows_t)
+    )(part, old, kernel_cols, rows_t)
 
 
 def sum_kernel(hist, rows, dom, parts, own, spots, momentum, out, got, mine, from_low, from_high, to_high, to_low,
@@ -457,9 +477,9 @@
     band = history.shape[1]
     width = kernel_cols.shape[1]
     spots, part = deposit(row_index, col_index, bin_index, charge.astype(jnp.float32)[None], rows, dom, band, width)
-    new = newest_grids(part, history, hist, rows, dom)
     rows_t = jnp.transpose(kernel_rows, (0, 2, 1, 3))
-    parts, own, cycle_now = field_parts(new, history, kernel_cols, rows_t, rows)
+    parts, own, newest = field_parts(part, history, kernel_cols, rows_t, hist, rows, dom)
+    cycle_now = jnp.concatenate([newest, history[:-STEPS]], axis=0)
     return sum_and_kick(parts, own, spots, momentum, hist, rows, dom), cycle_now
 
 

time: 102 us -> 93 us (0.912)
  Pallas kernels: 93.3 us -> 83.7 us
  other arithmetic: 1.28 us -> 2.78 us
    pallas_call x2 -> x1, Pallas kernels: 36.1 us -> 25.6 us  [field_parts(): pl.pallas_call(functools.partial(field_kernel, hist, rows, dom), out_shap...]
    concatenate x0 -> x1, other arithmetic: none -> 1.5 us  [local(): cycle_now = jnp.concatenate([newest, history[:-STEPS]], axis=0)]
    unnamed x2 -> x6, local copies, waits for them, and re-layouts: 6.27 us -> 5.58 us
where the time goes in v2:
time: 93 us; the launch traced here: 92.7 us
  Pallas kernels  83.7 us (90%)
  local copies, waits for them, and re-layouts  5.59 us (6%)
  other arithmetic  2.78 us (3%)
    pallas_call x1, Pallas kernels, sum_and_kick(): pl.pallas_call(functools.partial(sum_kernel, hist, rows, dom), out_shape=...  43.9 us
    pallas_call x1, Pallas kernels, field_parts(): pl.pallas_call(functools.partial(field_kernel, hist, rows, dom), out_shap...  25.6 us
    pallas_call x1, Pallas kernels, deposit(): pl.pallas_call(functools.partial(gather_kernel, rows, dom), out_shape=(ja...  14.1 us
    unnamed x6, local copies, waits for them, and re-layouts  5.58 us

profile of v2, /device:TPU:0, one launch (start us, length us, event | category | flops | bytes accessed | tf_op | source)
XLA Modules:
  0.0 92.7 jit_solution(10987796925005502606)
XLA Ops:
  0.6 1.3 %broadcast_in_dim.7 = f32[1024]{0:T(1024)} convert(bf16[1024]{0:T(1024)(128)(2,1)} %param.11) | non-fusion elementwise | flops 1024 | bytes 6144 | tf_op jit(solution)/shard_map/broadcast_in_dim | solution.py:479
  1.9 14.1 %shard_map.95 = (f32[8,8,1024]{2,1,0:T(8,128)}, bf16[4,256,128]{2,1,0:T(8,128)(2,1)}) custom-call(s32[4,1024]{1,0:T(4,128)} %row_ref.1, s32[4,1024]{1,0:T(4,128)} %col_ref.1, s32[4,1024]{1,0:T(4,128)} %bin_ref.1, f32[1,1024]{1,0:T(1,128)} %bitcast.5), custom_call_target="tpu_custom_call" | custom-call | tf_op jit(solution)/shard_map/pallas_call | solution.py:97
  16.1 5.0 %copy.12 = bf16[8,256,2,512]{3,1,2,0:T(8,128)(2,1)} copy(bf16[8,256,2,512]{3,2,1,0:T(2,128)(2,1)} %param.15) | data formatting | bytes 8388608 | tf_op args[7]
  21.0 25.6 %shard_map.96 = (bf16[2,512,512]{2,1,0:T(8,128)(2,1)}, f32[512,512]{1,0:T(8,128)}, bf16[4,256,512]{2,1,0:T(8,128)(2,1)}) custom-call(bf16[4,256,128]{2,1,0:T(8,128)(2,1)} %get-tuple-element.7.part, bf16[8,256,512]{2,1,0:T(8,128)(2,1)} %old_ref.1, bf16[8,128,512]{2,1,0:T(8,128)(2,1)} %cols_ref.1, bf16[8,2,256,512]{3,2,1,0:T(8,128)(2,1)} %bitcast.4), custom_call_target="tpu_custom_call" | custom-call | tf_op jit(solution)/shard_map/pallas_call | solution.py:277
  46.7 0.0 slice-start
  46.7 0.0 copy-start
  46.7 43.9 %shard_map.97 = f32[2,1024]{1,0:T(2,128)} custom-call(bf16[2,512,512]{2,1,0:T(8,128)(2,1)} %get-tuple-element.8.parts, f32[512,512]{1,0:T(8,128)} %get-tuple-element.9.own, f32[8,8,1024]{2,1,0:T(8,128)} %get-tuple-element.10.spots, f32[2,1024]{1,0:T(2,128)} %momentum.1), custom_call_target="tpu_custom_call" | custom-call | tf_op jit(solution)/shard_map/pallas_call | solution.py:465
  90.6 0.0 slice-done
  90.6 0.0 copy-done
  90.6 0.0 copy-start.1
  90.6 1.5 %pad_maximum_fusion = bf16[8,256,512]{2,1,0:T(8,128)(2,1)} fusion(bf16[4,256,512]{2,1,0:T(8,128)(2,1)S(1)} %slice-done, bf16[4,256,512]{2,1,0:T(8,128)(2,1)S(1)} %copy-done), kind=kLoop, calls=%fused_computation.1 | loop fusion | flops 1048576 | bytes 4194304 | tf_op jit(solution)/shard_map/concatenate | solution.py:482
  92.1 0.0 copy-done.1
  92.1 0.6 copy.14
Async XLA Ops:
  46.7 43.9 %slice-start = ((bf16[8,256,512]{2,1,0:T(8,128)(2,1)}), bf16[4,256,512]{2,1,0:T(8,128)(2,1)S(1)}, s32[]{:S(2)}) async-start(bf16[8,256,512]{2,1,0:T(8,128)(2,1)} %old_ref.1), calls=%async_computation | async-start | bytes 2097152 | tf_op jit(solution)/shard_map/slice | solution.py:482
  46.7 43.9 %copy-start = (bf16[4,256,512]{2,1,0:T(8,128)(2,1)S(1)}, bf16[4,256,512]{2,1,0:T(8,128)(2,1)}, u32[]{:S(2)}) copy-start(bf16[4,256,512]{2,1,0:T(8,128)(2,1)} %get-tuple-element.11) | copy-start | bytes 3145732
  90.6 1.5 %copy-start.1 = (f32[2,1024]{1,0:T(2,128)S(1)}, f32[2,1024]{1,0:T(2,128)}, u32[]{:S(2)}) copy-start(f32[2,1024]{1,0:T(2,128)} %shard_map.97) | copy-start | bytes 24580

commit v3 on v2

--- a/solution.py
+++ b/solution.py
@@ -359,10 +359,11 @@
                 kicks[k, comp:comp + 1, :] += jnp.sum(both * col, axis=0, keepdims=True)
             return carry
 
-        lax.fori_loop(0, n, block, 0)
+        lax.fori_loop(0, n, block, 0, unroll=8)
 
     lag = 2 * (hist - 2)
     group = PIECES // STEPS
+    late = lag + 3
 
     def step(t, carry):
         @pl.when(t < PIECES)
@@ -399,7 +400,7 @@
             to_low[span(high)] = (mine[span(high)] + from_high[span(high)].astype(jnp.float32)).astype(kind)
             down_copy(high).start()
 
-        done = t - lag
+        done = t - late
 
         @pl.when(done >= 0)
         def _():
@@ -424,7 +425,7 @@
 
         return carry
 
-    lax.fori_loop(0, PIECES + lag, step, 0)
+    lax.fori_loop(0, PIECES + late, step, 0)
 
     def kick_copy(k):
         _, device = plane_peer(rows, dom, n - k)

time: 93 us -> 87.1 us (0.937)
  Pallas kernels: 83.7 us -> 77.7 us
    pallas_call x1, Pallas kernels: 43.9 us -> 38 us  [sum_and_kick(): pl.pallas_call(functools.partial(sum_kernel, hist, rows, dom), out_shape=...]
where the time goes in v3:
time: 87.1 us; the launch traced here: 86.8 us
  Pallas kernels  77.7 us (89%)
  local copies, waits for them, and re-layouts  5.59 us (6%)
  other arithmetic  2.78 us (3%)
    pallas_call x1, Pallas kernels, sum_and_kick(): pl.pallas_call(functools.partial(sum_kernel, hist, rows, dom), out_shape=...  38 us
    pallas_call x1, Pallas kernels, field_parts(): pl.pallas_call(functools.partial(field_kernel, hist, rows, dom), out_shap...  25.6 us
    pallas_call x1, Pallas kernels, deposit(): pl.pallas_call(functools.partial(gather_kernel, rows, dom), out_shape=(ja...  14.1 us
    unnamed x6, local copies, waits for them, and re-layouts  5.58 us

profile of v3, /device:TPU:0, one launch (start us, length us, event | category | flops | bytes accessed | tf_op | source)
XLA Modules:
  0.0 86.8 jit_solution(1732792044567915365)
XLA Ops:
  0.6 1.3 %broadcast_in_dim.7 = f32[1024]{0:T(1024)} convert(bf16[1024]{0:T(1024)(128)(2,1)} %param.11) | non-fusion elementwise | flops 1024 | bytes 6144 | tf_op jit(solution)/shard_map/broadcast_in_dim | solution.py:480
  1.9 14.1 %shard_map.95 = (f32[8,8,1024]{2,1,0:T(8,128)}, bf16[4,256,128]{2,1,0:T(8,128)(2,1)}) custom-call(s32[4,1024]{1,0:T(4,128)} %row_ref.1, s32[4,1024]{1,0:T(4,128)} %col_ref.1, s32[4,1024]{1,0:T(4,128)} %bin_ref.1, f32[1,1024]{1,0:T(1,128)} %bitcast.5), custom_call_target="tpu_custom_call" | custom-call | tf_op jit(solution)/shard_map/pallas_call | solution.py:97
  16.1 5.0 %copy.12 = bf16[8,256,2,512]{3,1,2,0:T(8,128)(2,1)} copy(bf16[8,256,2,512]{3,2,1,0:T(2,128)(2,1)} %param.15) | data formatting | bytes 8388608 | tf_op args[7]
  21.0 25.6 %shard_map.96 = (bf16[2,512,512]{2,1,0:T(8,128)(2,1)}, f32[512,512]{1,0:T(8,128)}, bf16[4,256,512]{2,1,0:T(8,128)(2,1)}) custom-call(bf16[4,256,128]{2,1,0:T(8,128)(2,1)} %get-tuple-element.7.part, bf16[8,256,512]{2,1,0:T(8,128)(2,1)} %old_ref.1, bf16[8,128,512]{2,1,0:T(8,128)(2,1)} %cols_ref.1, bf16[8,2,256,512]{3,2,1,0:T(8,128)(2,1)} %bitcast.4), custom_call_target="tpu_custom_call" | custom-call | tf_op jit(solution)/shard_map/pallas_call | solution.py:277
  46.7 0.0 slice-start
  46.7 0.0 copy-start
  46.7 38.0 %shard_map.97 = f32[2,1024]{1,0:T(2,128)} custom-call(bf16[2,512,512]{2,1,0:T(8,128)(2,1)} %get-tuple-element.8.parts, f32[512,512]{1,0:T(8,128)} %get-tuple-element.9.own, f32[8,8,1024]{2,1,0:T(8,128)} %get-tuple-element.10.spots, f32[2,1024]{1,0:T(2,128)} %momentum.1), custom_call_target="tpu_custom_call" | custom-call | tf_op jit(solution)/shard_map/pallas_call | solution.py:466
  84.7 0.0 slice-done
  84.7 0.0 copy-done
  84.7 0.0 copy-start.1
  84.7 1.5 %pad_maximum_fusion = bf16[8,256,512]{2,1,0:T(8,128)(2,1)} fusion(bf16[4,256,512]{2,1,0:T(8,128)(2,1)S(1)} %slice-done, bf16[4,256,512]{2,1,0:T(8,128)(2,1)S(1)} %copy-done), kind=kLoop, calls=%fused_computation.1 | loop fusion | flops 1048576 | bytes 4194304 | tf_op jit(solution)/shard_map/concatenate | solution.py:483
  86.2 0.0 copy-done.1
  86.2 0.6 copy.14
Async XLA Ops:
  46.7 38.0 %slice-start = ((bf16[8,256,512]{2,1,0:T(8,128)(2,1)}), bf16[4,256,512]{2,1,0:T(8,128)(2,1)S(1)}, s32[]{:S(2)}) async-start(bf16[8,256,512]{2,1,0:T(8,128)(2,1)} %old_ref.1), calls=%async_computation | async-start | bytes 2097152 | tf_op jit(solution)/shard_map/slice | solution.py:483
  46.7 38.0 %copy-start = (bf16[4,256,512]{2,1,0:T(8,128)(2,1)S(1)}, bf16[4,256,512]{2,1,0:T(8,128)(2,1)}, u32[]{:S(2)}) copy-start(bf16[4,256,512]{2,1,0:T(8,128)(2,1)} %get-tuple-element.11) | copy-start | bytes 3145732
  84.7 1.5 %copy-start.1 = (f32[2,1024]{1,0:T(2,128)S(1)}, f32[2,1024]{1,0:T(2,128)}, u32[]{:S(2)}) copy-start(f32[2,1024]{1,0:T(2,128)} %shard_map.97) | copy-start | bytes 24580
